TPU v7x, 128 devices: a whole 4x4x4 slice. The times are simulated.
128 devices in a mesh: fsdp: 32 (over z, y, x_hi), sp: 4 (over x_lo, core).
Axes of the slice: x: 4 (x_hi: 2, x_lo: 2; x = x_hi * 2 + x_lo), y: 4, z: 4, core: 2. Of those that a mesh axis runs over, the one named last changes fastest.
Arguments:
- tokens: bfloat16 [32, 512, 1536], P('fsdp', 'sp'), may hold values from -6 to 6
- modulation: float32 [32, 1, 6, 1536], P('fsdp'), may hold values from -4 to 4
- w_qkv: bfloat16 [1, 1536, 3, 1536], P(None, 'fsdp', None, 'sp'), may hold values from -0.15625 to 0.15625
- w_out: bfloat16 [1, 1536, 1536], P(None, 'sp', 'fsdp'), may hold values from -0.15625 to 0.15625
- w_in: bfloat16 [1, 1536, 6144], P(None, 'fsdp', 'sp'), may hold values from -0.15625 to 0.15625
- w_back: bfloat16 [1, 6144, 1536], P(None, 'sp', 'fsdp'), may hold values from -0.078125 to 0.078125
- out_grad: bfloat16 [32, 512, 1536], P('fsdp', 'sp'), may hold values from -6 to 6
Outputs:
- final_out: bfloat16 [32, 512, 1536], P('fsdp', 'sp')
- input_grad: float32 [32, 512, 1536], P('fsdp', 'sp')
- grad_qkv: float32 [1, 1536, 3, 1536], P(None, 'fsdp', None, 'sp')
- grad_out: float32 [1, 1536, 1536], P(None, 'sp', 'fsdp')
- grad_in: float32 [1, 1536, 6144], P(None, 'fsdp', 'sp')
- grad_back: float32 [1, 6144, 1536], P(None, 'sp', 'fsdp')
All inputs are finite; a program needn't handle non-finite values.
Results may differ from a plain program's by a relative error of at most 0.03.
Values may be sent and summed in bfloat16 or wider, within the bound.
A program may use at most 128 MiB of HBM per device.

v0:
```python
import math
import jax
import jax.numpy as jnp
from jax import lax
from jax.sharding import PartitionSpec as P

HEAD_DIM = 128
LN_EPS = 1e-06
TEMPER = 2.5


def normalize(x):
    c = x - jnp.mean(x, axis=-1, keepdims=True)
    r = lax.rsqrt(jnp.mean(c * c, axis=-1, keepdims=True) + LN_EPS)
    return (c * r, r)


def norm_back(n, r, e):
    return r * (
        e - jnp.mean(e, axis=-1, keepdims=True) - n * jnp.mean(e * n, axis=-1, keepdims=True)
    )


def dot(a, b, ca, cb):
    return lax.dot_general(a, b, (((ca,), (cb,)), ((), ())), preferred_element_type=jnp.float32)


def bf(x):
    return x.astype(jnp.bfloat16)


def body(tokens, modulation, w_qkv, w_out, w_in, w_back, out_grad):
    seq, width = tokens.shape[1:]
    own = w_qkv.shape[3]
    heads = own // HEAD_DIM
    ff = w_in.shape[2]
    c = TEMPER / math.sqrt(HEAD_DIM)
    q_s = 1.0 / math.sqrt(seq * lax.axis_size("fsdp") * lax.axis_size("sp"))
    mod = modulation[0, 0]
    m = [mod[i : i + 1] for i in range(6)]
    rows = w_qkv.shape[1]
    weights = [
        lax.all_gather(w, "fsdp", axis=0, tiled=True)
        for w in (w_qkv[0].reshape(rows, 3 * own), w_out[0].T, w_in[0], w_back[0].T)
    ]
    wq, wo, wi, wb = weights

    def gather(v):
        return lax.all_gather(v, "sp", axis=0, tiled=True)

    def scatter(v):
        return lax.psum_scatter(bf(v), "sp", scatter_dimension=0, tiled=True).astype(jnp.float32)

    x = tokens[0].astype(jnp.float32)
    dx = out_grad[0].astype(jnp.float32)
    n1, r1 = normalize(x)
    a1 = gather(bf(n1 * (1.0 + m[1]) + m[0]))
    dm = gather(bf(m[5] * dx))
    qkv = bf(dot(a1, wq, 1, 0))

    def attend(h):
        q, k, v = (qkv[:, i * own + h * HEAD_DIM : i * own + (h + 1) * HEAD_DIM] for i in range(3))
        p = jax.nn.softmax(dot(q, k, 1, 1) * c, axis=-1)
        return (q, k, v, p)

    o = jnp.concatenate(
        [bf(dot(bf(p), v, 1, 0)) for q, k, v, p in map(attend, range(heads))], axis=1
    )
    mid = x + m[2] * scatter(dot(o, wo, 1, 1))
    n2, r2 = normalize(mid)
    a2 = gather(bf(n2 * (1.0 + m[4]) + m[3]))
    u = dot(a2, wi, 1, 0)
    act, pull = jax.vjp(lambda t: jax.nn.gelu(t, approximate=True), u)
    g = bf(act)
    final = bf(mid + m[5] * scatter(dot(g, wb, 1, 1)))
    du = bf(pull(dot(dm, wb, 1, 0))[0])
    dmid = dx + norm_back(n2, r2, scatter(dot(du, wi, 1, 1)) * (1.0 + m[4]))
    da = gather(bf(m[2] * dmid))
    do = bf(dot(da, wo, 1, 0))
    dq, dk, dv = ([], [], [])
    for h in range(heads):
        q, k, v, p = attend(h)
        doh = do[:, h * HEAD_DIM : (h + 1) * HEAD_DIM]
        dp = dot(doh, v, 1, 1)
        ds = bf(c * p * (dp - jnp.sum(p * dp, axis=-1, keepdims=True)))
        dq.append(bf(dot(ds, k, 1, 0)))
        dk.append(bf(dot(ds, q, 0, 0)))
        dv.append(bf(dot(bf(p), doh, 0, 0)))
    dqkv = jnp.concatenate(dq + dk + dv, axis=1)
    dxin = dmid + norm_back(n1, r1, scatter(dot(dqkv, wq, 1, 1)) * (1.0 + m[1]))

    def reduce(a, b):
        g = bf(dot(a, b, 0, 0) * q_s)
        return lax.psum_scatter(g, "fsdp", scatter_dimension=0, tiled=True).astype(jnp.float32)

    gb = reduce(dm, g)
    gi = reduce(a2, du)
    go = reduce(da, o)
    gq = reduce(a1, dqkv)
    return (final[None], dxin[None], gq.reshape(1, rows, 3, own), go.T[None], gi[None], gb.T[None])


def solution(mesh):
    return jax.shard_map(
        body,
        mesh=mesh,
        in_specs=(
            P("fsdp", "sp", None),
            P("fsdp", None, None, None),
            P(None, "fsdp", None, "sp"),
            P(None, "sp", "fsdp"),
            P(None, "fsdp", "sp"),
            P(None, "sp", "fsdp"),
            P("fsdp", "sp", None),
        ),
        out_specs=(
            P("fsdp", "sp", None),
            P("fsdp", "sp", None),
            P(None, "fsdp", None, "sp"),
            P(None, "sp", "fsdp"),
            P(None, "fsdp", "sp"),
            P(None, "sp", "fsdp"),
        ),
        check_vma=False,
    )
```

profile of v0, /device:TPU:0, one launch (start us, length us, event | category | flops | bytes accessed | tf_op | source)
XLA Modules:
  0.0 1512.2 jit_solution(13099963642387650823)
XLA Ops:
  14.2 25.6 %all-gather.10.cloned.1.call-done = bf16[512,1536]{1,0:T(8,128)(2,1)} async-done(((bf16[128,1536]{1,0:T(8,128)(2,1)}), bf16[512,1536]{1,0:T(8,128)(2,1)}) %all-gather.10.cloned.1.call-update) | async-done | bytes 1572880 | tf_op jit(solution)/shard_map/all_gather | solution.py:49
  39.8 81.9 %all-gather.12.cloned.1.call-done = bf16[1536,1152]{1,0:T(8,128)(2,1)} async-done(((bf16[48,1152]{1,0:T(8,128)(2,1)}), bf16[1536,1152]{1,0:T(8,128)(2,1)}) %all-gather.12.cloned.1.call-update) | async-done | bytes 3538960 | tf_op jit(solution)/shard_map/all_gather | solution.py:43
  121.7 4.7 convolution_convert_fusion.1
  129.1 61.7 %all-gather.14.cloned.1.call-done = bf16[1536,384]{1,0:T(8,128)(2,1)} async-done(((bf16[48,384]{1,0:T(8,128)(2,1)}), bf16[1536,384]{1,0:T(8,128)(2,1)}) %all-gather.14.cloned.1.call-update) | async-done | bytes 1179664 | tf_op jit(solution)/shard_map/all_gather | solution.py:43
  197.4 18.1 %reduce-scatter.9.cloned.1.call-done = bf16[128,1536]{1,0:T(8,128)(2,1)} async-done(((bf16[512,1536]{1,0:T(8,128)(2,1)}), bf16[128,1536]{1,0:T(8,128)(2,1)}) %reduce-scatter.9.cloned.1.call-update) | async-done | bytes 393232 | tf_op jit(solution)/shard_map/reduce_scatter | solution.py:52
  219.2 24.0 %all-gather.20.cloned.1.call-done = bf16[512,1536]{1,0:T(8,128)(2,1)} async-done(((bf16[128,1536]{1,0:T(8,128)(2,1)}), bf16[512,1536]{1,0:T(8,128)(2,1)}) %all-gather.20.cloned.1.call-update) | async-done | bytes 1572880 | tf_op jit(solution)/shard_map/all_gather | solution.py:49
  243.1 86.9 %all-gather.18.cloned.1.call-done = bf16[1536,1536]{1,0:T(8,128)(2,1)} async-done(((bf16[48,1536]{1,0:T(8,128)(2,1)}), bf16[1536,1536]{1,0:T(8,128)(2,1)}) %all-gather.18.cloned.1.call-update) | async-done | bytes 4718608 | tf_op jit(solution)/shard_map/all_gather | solution.py:43
  330.0 7.1 fusion.97
  337.2 77.5 %all-gather.24.cloned.1.call-done = bf16[1,1536,1536]{2,1,0:T(8,128)(2,1)} async-done(((bf16[1,48,1536]{2,1,0:T(8,128)(2,1)}), bf16[1,1536,1536]{2,1,0:T(8,128)(2,1)}) %all-gather.24.cloned.1.call-update) | async-done | bytes 4718608 | tf_op jit(solution)/shard_map/all_gather | solution.py:43
  414.7 25.5 %all-gather.16.cloned.1.call-done = bf16[512,1536]{1,0:T(8,128)(2,1)} async-done(((bf16[128,1536]{1,0:T(8,128)(2,1)}), bf16[512,1536]{1,0:T(8,128)(2,1)}) %all-gather.16.cloned.1.call-update) | async-done | bytes 1572880 | tf_op jit(solution)/shard_map/all_gather | solution.py:49
  440.2 9.7 fusion.13
  451.1 3.8 fusion.14
  455.2 7.3 convolution_convert_fusion.2
  462.6 17.5 %reduce-scatter.13.cloned.1.call-done = bf16[128,1536]{1,0:T(8,128)(2,1)} async-done(((bf16[512,1536]{1,0:T(8,128)(2,1)}), bf16[128,1536]{1,0:T(8,128)(2,1)}) %reduce-scatter.13.cloned.1.call-update) | async-done | bytes 393232 | tf_op jit(solution)/shard_map/reduce_scatter | solution.py:52
  481.5 25.7 %reduce-scatter.11.cloned.1.call-done = bf16[128,1536]{1,0:T(8,128)(2,1)} async-done(((bf16[512,1536]{1,0:T(8,128)(2,1)}), bf16[128,1536]{1,0:T(8,128)(2,1)}) %reduce-scatter.11.cloned.1.call-update) | async-done | bytes 393232 | tf_op jit(solution)/shard_map/reduce_scatter | solution.py:52
  510.1 25.6 %all-gather.22.cloned.1.call-done = bf16[512,1536]{1,0:T(8,128)(2,1)} async-done(((bf16[128,1536]{1,0:T(8,128)(2,1)}), bf16[512,1536]{1,0:T(8,128)(2,1)}) %all-gather.22.cloned.1.call-update) | async-done | bytes 1572880 | tf_op jit(solution)/shard_map/all_gather | solution.py:49
  562.1 4.4 fusion
  567.9 6.8 fusion.1
  576.4 4.1 fusion.2
  580.5 196.6 %reduce-scatter.19.cloned.1.call-done = bf16[48,384]{1,0:T(8,128)(2,1)} async-done(((bf16[1536,384]{1,0:T(8,128)(2,1)}), bf16[48,384]{1,0:T(8,128)(2,1)}) %reduce-scatter.19.cloned.1.call-update) | async-done | bytes 36880 | tf_op jit(solution)/shard_map/reduce_scatter | solution.py:94
  778.6 21.9 %reduce-scatter.15.cloned.1.call-done = bf16[128,1536]{1,0:T(8,128)(2,1)} async-done(((bf16[512,1536]{1,0:T(8,128)(2,1)}), bf16[128,1536]{1,0:T(8,128)(2,1)}) %reduce-scatter.15.cloned.1.call-update) | async-done | bytes 393232 | tf_op jit(solution)/shard_map/reduce_scatter | solution.py:52
  804.0 234.6 %reduce-scatter.21.cloned.1.call-done = bf16[48,1536]{1,0:T(8,128)(2,1)} async-done(((bf16[1536,1536]{1,0:T(8,128)(2,1)}), bf16[48,1536]{1,0:T(8,128)(2,1)}) %reduce-scatter.21.cloned.1.call-update) | async-done | bytes 147472 | tf_op jit(solution)/shard_map/reduce_scatter | solution.py:94
  1040.2 232.4 %reduce-scatter.23.cloned.1.call-done = bf16[48,1536]{1,0:T(8,128)(2,1)} async-done(((bf16[1536,1536]{1,0:T(8,128)(2,1)}), bf16[48,1536]{1,0:T(8,128)(2,1)}) %reduce-scatter.23.cloned.1.call-update) | async-done | bytes 147472 | tf_op jit(solution)/shard_map/reduce_scatter | solution.py:94
  1274.2 229.8 %reduce-scatter.17.cloned.1.call-done = bf16[48,1152]{1,0:T(8,128)(2,1)} async-done(((bf16[1536,1152]{1,0:T(8,128)(2,1)}), bf16[48,1152]{1,0:T(8,128)(2,1)}) %reduce-scatter.17.cloned.1.call-update) | async-done | bytes 110608 | tf_op jit(solution)/shard_map/reduce_scatter | solution.py:94
  (178 shorter events, 64.6 us)
Async XLA Ops:
  7.2 32.6 %all-gather.10.cloned.1.call-start = ((), (), s32[]{:S(2)}) async-start(), calls=%async_computation.8 | async-start | bytes 1966080 | tf_op jit(solution)/shard_map/all_gather | solution.py:49
  8.4 118.0 %copy-start.22 = (f32[128]{0:T(128)}, f32[128]{0:T(128)S(1)}, u32[]{:S(2)}) copy-start(f32[128]{0:T(128)S(1)} %broadcast_multiply_fusion.5) | copy-start | bytes 1540
  9.6 116.7 %copy-start.24 = (f32[128]{0:T(128)}, f32[128]{0:T(128)S(1)}, u32[]{:S(2)}) copy-start(f32[128]{0:T(128)S(1)} %add_rsqrt_fusion.1) | copy-start | bytes 1540
  12.6 109.1 %all-gather.12.cloned.1.call-start = ((), (), s32[]{:S(2)}) async-start(), calls=%async_computation.9 | async-start | bytes 3649536 | tf_op jit(solution)/shard_map/all_gather | solution.py:43
  13.4 177.3 %all-gather.14.cloned.1.call-start = ((), (), s32[]{:S(2)}) async-start(), calls=%async_computation.10 | async-start | bytes 1216512 | tf_op jit(solution)/shard_map/all_gather | solution.py:43
  14.1 201.4 %reduce-scatter.9.cloned.1.call-start = ((), (), s32[]{:S(2)}) async-start(), calls=%async_computation.11 | async-start | bytes 1966080 | tf_op jit(solution)/shard_map/reduce_scatter | solution.py:52
  126.9 411.6 %copy-start.14 = (f32[512]{0:T(512)}, f32[512]{0:T(512)S(1)}, u32[]{:S(2)}) copy-start(f32[512]{0:T(512)S(1)} %fusion.39) | copy-start | bytes 6148
  128.3 62.4 %copy-start.36 = (bf16[512,128]{0,1:T(8,128)(2,1)}, bf16[512,128]{0,1:T(8,128)(2,1)S(1)}, u32[]{:S(2)}) copy-start(bf16[512,128]{0,1:T(8,128)(2,1)S(1)} %convolution_convert_fusion.14) | copy-start | bytes 393220
  128.7 62.0 %copy-start.38 = (bf16[512,128]{0,1:T(8,128)(2,1)}, bf16[512,128]{0,1:T(8,128)(2,1)S(1)}, u32[]{:S(2)}) copy-start(bf16[512,128]{0,1:T(8,128)(2,1)S(1)} %convolution_convert_fusion.15) | copy-start | bytes 393220
  194.2 48.9 %all-gather.20.cloned.1.call-start = ((), (), s32[]{:S(2)}) async-start(), calls=%async_computation.15 | async-start | bytes 1966080 | tf_op jit(solution)/shard_map/all_gather | solution.py:49
  196.0 134.0 %all-gather.18.cloned.1.call-start = ((), (), s32[]{:S(2)}) async-start(), calls=%async_computation.13 | async-start | bytes 4866048 | tf_op jit(solution)/shard_map/all_gather | solution.py:43
  196.6 218.1 %all-gather.24.cloned.1.call-start = ((), (), s32[]{:S(2)}) async-start(), calls=%async_computation.23 | async-start | bytes 4866048 | tf_op jit(solution)/shard_map/all_gather | solution.py:43
  197.4 242.8 %all-gather.16.cloned.1.call-start = ((), (), s32[]{:S(2)}) async-start(), calls=%async_computation.12 | async-start | bytes 1966080 | tf_op jit(solution)/shard_map/all_gather | solution.py:49
  219.1 261.0 %reduce-scatter.13.cloned.1.call-start = ((), (), s32[]{:S(2)}) async-start(), calls=%async_computation.16 | async-start | bytes 1966080 | tf_op jit(solution)/shard_map/reduce_scatter | solution.py:52
  455.0 52.2 %reduce-scatter.11.cloned.1.call-start = ((), (), s32[]{:S(2)}) async-start(), calls=%async_computation.14 | async-start | bytes 1966080 | tf_op jit(solution)/shard_map/reduce_scatter | solution.py:52
  462.5 73.2 %all-gather.22.cloned.1.call-start = ((), (), s32[]{:S(2)}) async-start(), calls=%async_computation.17 | async-start | bytes 1966080 | tf_op jit(solution)/shard_map/all_gather | solution.py:49
  510.1 267.1 %reduce-scatter.19.cloned.1.call-start = ((), (), s32[]{:S(2)}) async-start(), calls=%async_computation.20 | async-start | bytes 1216512 | tf_op jit(solution)/shard_map/reduce_scatter | solution.py:94
  549.3 251.2 %reduce-scatter.15.cloned.1.call-start = ((), (), s32[]{:S(2)}) async-start(), calls=%async_computation.18 | async-start | bytes 1966080 | tf_op jit(solution)/shard_map/reduce_scatter | solution.py:52
  560.7 477.8 %reduce-scatter.21.cloned.1.call-start = ((), (), s32[]{:S(2)}) async-start(), calls=%async_computation.21 | async-start | bytes 4866048 | tf_op jit(solution)/shard_map/reduce_scatter | solution.py:94
  566.5 706.1 %reduce-scatter.23.cloned.1.call-start = ((), (), s32[]{:S(2)}) async-start(), calls=%async_computation.22 | async-start | bytes 4866048 | tf_op jit(solution)/shard_map/reduce_scatter | solution.py:94
  574.7 929.3 %reduce-scatter.17.cloned.1.call-start = ((), (), s32[]{:S(2)}) async-start(), calls=%async_computation.19 | async-start | bytes 3649536 | tf_op jit(solution)/shard_map/reduce_scatter | solution.py:94
  580.5 220.0 %copy-start.23 = (f32[128]{0:T(128)S(1)}, f32[128]{0:T(128)}, u32[]{:S(2)}) copy-start(f32[128]{0:T(128)} %copy-done.22) | copy-start | bytes 1540
  580.5 220.0 %copy-start.25 = (f32[128]{0:T(128)S(1)}, f32[128]{0:T(128)}, u32[]{:S(2)}) copy-start(f32[128]{0:T(128)} %copy-done.24) | copy-start | bytes 1540
  580.5 221.3 %copy-start.4 = (f32[128,1536]{1,0:T(8,128)S(1)}, f32[128,1536]{1,0:T(8,128)}, u32[]{:S(2)}) copy-start(f32[128,1536]{1,0:T(8,128)} %get-tuple-element.29) | copy-start | bytes 2359300
  (38 other events, 167.3 us)
Sparse Core Ops, SparseCore 0:
  12.7 27.0 all-gather.9
  43.4 78.2 all-gather.11
  124.7 65.9 all-gather.13
  194.3 21.1 reduce-scatter.8
  217.6 25.4 all-gather.19
  246.0 83.9 all-gather.17
  333.1 81.5 all-gather.23
  416.9 23.2 all-gather.15
  455.1 24.9 reduce-scatter.12
  482.3 24.7 reduce-scatter.10
  510.2 25.4 all-gather.21
  549.4 227.6 reduce-scatter.18
  779.6 20.8 reduce-scatter.14
  805.4 233.1 reduce-scatter.20
  1043.5 229.0 reduce-scatter.22
  1277.4 226.5 reduce-scatter.16
where the time goes:
time: 1510 us
  waiting for transfers between devices  1390 us (92%)
  matrix products  72.8 us (5%)
  other arithmetic  25 us (2%)
    reduce_scatter x4, waiting for transfers between devices, reduce(): lax.psum_scatter(g, 'fsdp', scatter_dimension=0, tiled=True)  893 us
    all_gather x4, waiting for transfers between devices, body(): lax.all_gather(w, 'fsdp', axis=0, tiled=True)  308 us
    all_gather x4, waiting for transfers between devices, gather(): return lax.all_gather(v, 'sp', axis=0, tiled=True)  101 us
    reduce_scatter x4, waiting for transfers between devices, scatter(): lax.psum_scatter(bf(v), 'sp', scatter_dimension=0, tiled=True)  83.3 us
    dot_general x30, matrix products, dot(): lax.dot_general(a, b, (((ca,), (cb,)), ((), ())), preferred_element_type=...  72.8 us
  transfers between devices with their start and end apart: 16, of which 16 were waited for; matrix products, arithmetic and copies ran while one was open for 4% of the time, Pallas kernels for 0%

commit v1 on v0

--- a/solution.py
+++ b/solution.py
@@ -7,6 +7,11 @@
 HEAD_DIM = 128
 LN_EPS = 1e-06
 TEMPER = 2.5
+
+
+def swapped_in(array, mesh_axis, along):
+    outgoing = jnp.stack([array] * lax.axis_size(mesh_axis))
+    return jnp.concatenate(lax.all_to_all(outgoing, mesh_axis, 0, 0), axis=along)
 
 
 def normalize(x):
@@ -40,7 +45,7 @@
     m = [mod[i : i + 1] for i in range(6)]
     rows = w_qkv.shape[1]
     weights = [
-        lax.all_gather(w, "fsdp", axis=0, tiled=True)
+        swapped_in(w, "fsdp", 0)
         for w in (w_qkv[0].reshape(rows, 3 * own), w_out[0].T, w_in[0], w_back[0].T)
     ]
     wq, wo, wi, wb = weights

time: 1510 us -> 1330 us (0.88)
  waiting for transfers between devices: 1390 us -> 1160 us
  starting transfers between devices: 1.06 us -> 26.4 us
    all_gather x4 -> x0, waiting for transfers between devices: 308 us -> none  [body(): lax.all_gather(w, 'fsdp', axis=0, tiled=True)]
    all_to_all x0 -> x4, waiting for transfers between devices: none -> 183 us  [swapped_in(): lax.all_to_all(outgoing, mesh_axis, 0, 0)]
    all_gather x4, waiting for transfers between devices: 101 us -> 25.6 us  [gather(): return lax.all_gather(v, 'sp', axis=0, tiled=True)]
    all_to_all x0 -> x4, starting transfers between devices: none -> 25.5 us  [swapped_in(): lax.all_to_all(outgoing, mesh_axis, 0, 0)]
    reduce_scatter x4, waiting for transfers between devices: 83.3 us -> 60.4 us  [scatter(): lax.psum_scatter(bf(v), 'sp', scatter_dimension=0, tiled=True)]
  transfers between devices with their start and end apart: 16 -> 16, of which waited for: 16 -> 12; matrix products, arithmetic and copies ran while one was open for 4% -> 6% of each run, Pallas kernels for 0% -> 0%
where the time goes in v1:
time: 1330 us
  waiting for transfers between devices  1160 us (87%)
  matrix products  83.4 us (6%)
  starting transfers between devices  26.4 us (2%)
  other arithmetic  23.5 us (2%)
  local copies, waits for them, and re-layouts  21.4 us (2%)
  between operations  14.9 us (1%)
    reduce_scatter x4, waiting for transfers between devices, reduce(): lax.psum_scatter(g, 'fsdp', scatter_dimension=0, tiled=True)  890 us
    all_to_all x4, waiting for transfers between devices, swapped_in(): lax.all_to_all(outgoing, mesh_axis, 0, 0)  183 us
    dot_general x30, matrix products, dot(): lax.dot_general(a, b, (((ca,), (cb,)), ((), ())), preferred_element_type=...  83.4 us
    reduce_scatter x4, waiting for transfers between devices, scatter(): lax.psum_scatter(bf(v), 'sp', scatter_dimension=0, tiled=True)  60.4 us
  transfers between devices with their start and end apart: 16, of which 12 were waited for; matrix products, arithmetic and copies ran while one was open for 6% of the time, Pallas kernels for 0%

profile of v1, /device:TPU:0, one launch (start us, length us, event | category | flops | bytes accessed | tf_op | source)
XLA Modules:
  0.0 1328.9 jit_solution(6505821571951696841)
XLA Ops:
  10.2 11.1 all-to-all-start
  23.6 56.4 %all-to-all-done = bf16[32,48,1152]{2,1,0:T(8,128)(2,1)} async-done(((bf16[32,48,1152]{2,1,0:T(8,128)(2,1)}), bf16[32,48,1152]{2,1,0:T(8,128)(2,1)}, u32[]{:S(2)}, u32[]{:S(2)}) %all-to-all-start) | async-done | bytes 3538976 | tf_op jit(solution)/shard_map/all_to_all | solution.py:14
  85.8 4.7 convolution_convert_fusion.1
  93.9 11.5 all-to-all-done.1
  109.0 4.9 all-to-all-start.3
  125.6 57.3 %all-to-all-done.3 = bf16[32,48,1536]{2,1,0:T(8,128)(2,1)} async-done(((bf16[32,48,1536]{2,1,0:T(8,128)(2,1)}), bf16[32,48,1536]{2,1,0:T(8,128)(2,1)}, u32[]{:S(2)}, u32[]{:S(2)}) %all-to-all-start.3) | async-done | bytes 4718624 | tf_op jit(solution)/shard_map/all_to_all | solution.py:14
  185.7 4.9 all-to-all-start.2
  194.5 7.0 fusion.90
  201.5 58.2 %all-to-all-done.2 = bf16[32,48,1536]{2,1,0:T(8,128)(2,1)} async-done(((bf16[32,48,1536]{2,1,0:T(8,128)(2,1)}), bf16[32,48,1536]{2,1,0:T(8,128)(2,1)}, u32[]{:S(2)}, u32[]{:S(2)}) %all-to-all-start.2) | async-done | bytes 4718624 | tf_op jit(solution)/shard_map/all_to_all | solution.py:14
  259.7 9.5 fusion.9
  270.4 6.1 convolution_convert_fusion.2
  276.6 7.3 convolution_convert_fusion.3
  283.9 12.7 reduce-scatter.13.cloned.1.call-done
  298.0 25.7 %reduce-scatter.11.cloned.1.call-done = bf16[128,1536]{1,0:T(8,128)(2,1)} async-done(((bf16[512,1536]{1,0:T(8,128)(2,1)}), bf16[128,1536]{1,0:T(8,128)(2,1)}) %reduce-scatter.11.cloned.1.call-update) | async-done | bytes 393232 | tf_op jit(solution)/shard_map/reduce_scatter | solution.py:57
  326.7 25.6 %all-gather.11.cloned.1.call-done = bf16[512,1536]{1,0:T(8,128)(2,1)} async-done(((bf16[128,1536]{1,0:T(8,128)(2,1)}), bf16[512,1536]{1,0:T(8,128)(2,1)}) %all-gather.11.cloned.1.call-update) | async-done | bytes 1572880 | tf_op jit(solution)/shard_map/all_gather | solution.py:54
  373.0 5.4 convolution_convert_fusion
  379.8 5.7 fusion
  386.9 6.9 fusion.1
  395.2 5.3 fusion.2
  400.6 193.1 %reduce-scatter.19.cloned.1.call-done = bf16[48,384]{1,0:T(8,128)(2,1)} async-done(((bf16[1536,384]{1,0:T(8,128)(2,1)}), bf16[48,384]{1,0:T(8,128)(2,1)}) %reduce-scatter.19.cloned.1.call-update) | async-done | bytes 36880 | tf_op jit(solution)/shard_map/reduce_scatter | solution.py:99
  595.0 21.9 %reduce-scatter.15.cloned.1.call-done = bf16[128,1536]{1,0:T(8,128)(2,1)} async-done(((bf16[512,1536]{1,0:T(8,128)(2,1)}), bf16[128,1536]{1,0:T(8,128)(2,1)}) %reduce-scatter.15.cloned.1.call-update) | async-done | bytes 393232 | tf_op jit(solution)/shard_map/reduce_scatter | solution.py:57
  620.5 234.5 %reduce-scatter.21.cloned.1.call-done = bf16[48,1536]{1,0:T(8,128)(2,1)} async-done(((bf16[1536,1536]{1,0:T(8,128)(2,1)}), bf16[48,1536]{1,0:T(8,128)(2,1)}) %reduce-scatter.21.cloned.1.call-update) | async-done | bytes 147472 | tf_op jit(solution)/shard_map/reduce_scatter | solution.py:99
  856.6 232.5 %reduce-scatter.23.cloned.1.call-done = bf16[48,1536]{1,0:T(8,128)(2,1)} async-done(((bf16[1536,1536]{1,0:T(8,128)(2,1)}), bf16[48,1536]{1,0:T(8,128)(2,1)}) %reduce-scatter.23.cloned.1.call-update) | async-done | bytes 147472 | tf_op jit(solution)/shard_map/reduce_scatter | solution.py:99
  1090.8 229.6 %reduce-scatter.17.cloned.1.call-done = bf16[48,1152]{1,0:T(8,128)(2,1)} async-done(((bf16[1536,1152]{1,0:T(8,128)(2,1)}), bf16[48,1152]{1,0:T(8,128)(2,1)}) %reduce-scatter.17.cloned.1.call-update) | async-done | bytes 110608 | tf_op jit(solution)/shard_map/reduce_scatter | solution.py:99
  (192 shorter events, 76.2 us)
Async XLA Ops:
  10.2 69.8 %all-to-all-start = ((bf16[32,48,1152]{2,1,0:T(8,128)(2,1)}), bf16[32,48,1152]{2,1,0:T(8,128)(2,1)}, u32[]{:S(2)}, u32[]{:S(2)}) async-start(bf16[32,48,1152]{2,1,0:T(8,128)(2,1)} %stack.8), calls=%async_computation | async-start | bytes 7077888 | tf_op jit(solution)/shard_map/all_to_all | solution.py:14
  21.3 58.7 %copy-start.13 = (bf16[1,384,48]{1,2,0:T(8,128)(2,1)S(1)}, bf16[1,384,48]{1,2,0:T(8,128)(2,1)}, u32[]{:S(2)}) copy-start(bf16[1,384,48]{1,2,0:T(8,128)(2,1)} %param.10) | copy-start | bytes 110596
  21.3 64.5 %all-gather.5.cloned.1.call-start = ((), (), s32[]{:S(2)}) async-start(), calls=%async_computation.12 | async-start | bytes 1966080 | tf_op jit(solution)/shard_map/all_gather | solution.py:54
  22.2 58.9 %copy-start.33 = (f32[128]{0:T(128)}, f32[128]{0:T(128)S(1)}, u32[]{:S(2)}) copy-start(f32[128]{0:T(128)S(1)} %broadcast_multiply_fusion.5) | copy-start | bytes 1540
  22.5 58.6 %copy-start.35 = (f32[128]{0:T(128)}, f32[128]{0:T(128)S(1)}, u32[]{:S(2)}) copy-start(f32[128]{0:T(128)S(1)} %add_rsqrt_fusion.1) | copy-start | bytes 1540
  81.1 24.3 %all-to-all-start.1 = ((bf16[32,48,384]{2,1,0:T(8,128)(2,1)}), bf16[32,48,384]{2,1,0:T(8,128)(2,1)}, u32[]{:S(2)}, u32[]{:S(2)}) async-start(bf16[32,48,384]{2,1,0:T(8,128)(2,1)} %stack.9), calls=%async_computation.1 | async-start | bytes 2359296 | tf_op jit(solution)/shard_map/all_to_all | solution.py:14
  109.0 73.9 %all-to-all-start.3 = ((bf16[32,48,1536]{2,1,0:T(8,128)(2,1)}), bf16[32,48,1536]{2,1,0:T(8,128)(2,1)}, u32[]{:S(2)}, u32[]{:S(2)}) async-start(bf16[32,48,1536]{2,1,0:T(8,128)(2,1)} %stack.11), calls=%async_computation.4 | async-start | bytes 9437184 | tf_op jit(solution)/shard_map/all_to_all | solution.py:14
  113.9 76.7 %reduce-scatter.9.cloned.1.call-start = ((), (), s32[]{:S(2)}) async-start(), calls=%async_computation.13 | async-start | bytes 1966080 | tf_op jit(solution)/shard_map/reduce_scatter | solution.py:57
  123.7 59.2 %copy-start.10 = (bf16[1,48,1536]{2,1,0:T(8,128)(2,1)S(1)}, bf16[1,48,1536]{2,1,0:T(8,128)(2,1)}, u32[]{:S(2)}) copy-start(bf16[1,48,1536]{2,1,0:T(8,128)(2,1)} %param.11) | copy-start | bytes 442372
  123.8 70.7 %all-gather.9.cloned.1.call-start = ((), (), s32[]{:S(2)}) async-start(), calls=%async_computation.16 | async-start | bytes 1966080 | tf_op jit(solution)/shard_map/all_gather | solution.py:54
  185.7 74.0 %all-to-all-start.2 = ((bf16[32,48,1536]{2,1,0:T(8,128)(2,1)}), bf16[32,48,1536]{2,1,0:T(8,128)(2,1)}, u32[]{:S(2)}, u32[]{:S(2)}) async-start(bf16[32,48,1536]{2,1,0:T(8,128)(2,1)} %stack.10), calls=%async_computation.3 | async-start | bytes 9437184 | tf_op jit(solution)/shard_map/all_to_all | solution.py:14
  190.6 69.1 %all-gather.7.cloned.1.call-start = ((), (), s32[]{:S(2)}) async-start(), calls=%async_computation.14 | async-start | bytes 1966080 | tf_op jit(solution)/shard_map/all_gather | solution.py:54
  194.2 102.4 %reduce-scatter.13.cloned.1.call-start = ((), (), s32[]{:S(2)}) async-start(), calls=%async_computation.17 | async-start | bytes 1966080 | tf_op jit(solution)/shard_map/reduce_scatter | solution.py:57
  276.5 47.2 %reduce-scatter.11.cloned.1.call-start = ((), (), s32[]{:S(2)}) async-start(), calls=%async_computation.15 | async-start | bytes 1966080 | tf_op jit(solution)/shard_map/reduce_scatter | solution.py:57
  283.9 68.4 %all-gather.11.cloned.1.call-start = ((), (), s32[]{:S(2)}) async-start(), calls=%async_computation.18 | async-start | bytes 1966080 | tf_op jit(solution)/shard_map/all_gather | solution.py:54
  326.6 28.4 %copy-start.18 = (f32[512]{0:T(512)S(1)}, f32[512]{0:T(512)}, u32[]{:S(2)}) copy-start(f32[512]{0:T(512)} %copy-done.16) | copy-start | bytes 6148
  326.6 267.0 %reduce-scatter.19.cloned.1.call-start = ((), (), s32[]{:S(2)}) async-start(), calls=%async_computation.21 | async-start | bytes 1216512 | tf_op jit(solution)/shard_map/reduce_scatter | solution.py:99
  365.8 251.2 %reduce-scatter.15.cloned.1.call-start = ((), (), s32[]{:S(2)}) async-start(), calls=%async_computation.19 | async-start | bytes 1966080 | tf_op jit(solution)/shard_map/reduce_scatter | solution.py:57
  378.4 476.6 %reduce-scatter.21.cloned.1.call-start = ((), (), s32[]{:S(2)}) async-start(), calls=%async_computation.22 | async-start | bytes 4866048 | tf_op jit(solution)/shard_map/reduce_scatter | solution.py:99
  385.5 703.6 %reduce-scatter.23.cloned.1.call-start = ((), (), s32[]{:S(2)}) async-start(), calls=%async_computation.23 | async-start | bytes 4866048 | tf_op jit(solution)/shard_map/reduce_scatter | solution.py:99
  393.8 926.6 %reduce-scatter.17.cloned.1.call-start = ((), (), s32[]{:S(2)}) async-start(), calls=%async_computation.20 | async-start | bytes 3649536 | tf_op jit(solution)/shard_map/reduce_scatter | solution.py:99
  400.5 216.5 %copy-start.34 = (f32[128]{0:T(128)S(1)}, f32[128]{0:T(128)}, u32[]{:S(2)}) copy-start(f32[128]{0:T(128)} %copy-done.33) | copy-start | bytes 1540
  400.5 216.5 %copy-start.36 = (f32[128]{0:T(128)S(1)}, f32[128]{0:T(128)}, u32[]{:S(2)}) copy-start(f32[128]{0:T(128)} %copy-done.35) | copy-start | bytes 1540
  400.5 217.8 %copy-start.4 = (f32[128,1536]{1,0:T(8,128)S(1)}, f32[128,1536]{1,0:T(8,128)}, u32[]{:S(2)}) copy-start(f32[128,1536]{1,0:T(8,128)} %get-tuple-element.29) | copy-start | bytes 2359300
  (45 other events, 157.3 us)
Sparse Core Ops, SparseCore 0:
  24.4 38.8 all-gather.4
  123.9 38.0 reduce-scatter.8
  164.2 26.0 all-gather.8
  194.4 39.0 all-gather.6
  276.6 19.9 reduce-scatter.12
  298.9 24.7 reduce-scatter.10
  326.7 25.4 all-gather.10
  365.9 227.6 reduce-scatter.18
  596.0 20.8 reduce-scatter.14
  621.9 233.0 reduce-scatter.20
  860.1 229.0 reduce-scatter.22
  1094.0 226.3 reduce-scatter.16
